TPU v7x, 32 devices: a whole 2x2x4 slice. The times are simulated.
32 devices in a mesh: heads: 4 (over y, core), batch: 8 (over z, x).
Axes of the slice: x: 2, y: 2, z: 4, core: 2. Of those that a mesh axis runs over, the one named last changes fastest.
Arguments:
- queries: bfloat16 [64, 4096], P('batch', 'heads'), may hold values from -6 to 6
- keys_new: bfloat16 [64, 4096], P('batch', 'heads'), may hold values from -6 to 6
- values_new: bfloat16 [64, 4096], P('batch', 'heads'), may hold values from -6 to 6
- out_gate: bfloat16 [64, 4096], P('batch', 'heads'), may hold values from -6 to 6
- decay_logit: float32 [64, 32], P('batch', 'heads'), may hold values from -6 to 6
- beta_logit: float32 [64, 32], P('batch', 'heads'), may hold values from -6 to 6
- decay_rate: float32 [32], P('heads'), may hold values from 0.05 to 2
- state: float32 [64, 32, 128, 128], P('batch', 'heads'), may hold values from -0.6 to 0.6
- norm_gain: float32 [128], replicated, may hold values from 0.1 to 1.9
- out_proj: bfloat16 [4096, 4096], P('heads'), may hold values from -0.09375 to 0.09375
- residual: bfloat16 [64, 4096], P('batch'), may hold values from -40 to 40, as said below
- final_gain: float32 [4096], replicated, may hold values from 0.1 to 1.9
- value_weight: float32 [4096], replicated, may hold values from -0.09375 to 0.09375
- lm_head: bfloat16 [4096, 4096], P(None, ('heads', 'batch')), may hold values from -15 to 15
- sampled: int32 [64], replicated, may hold values from 0 to 4095
Outputs:
- logprob: float32 [64], P('batch')
- value: float32 [64], P('batch')
Inputs may be any that keep to these rules, and one draw needn't show every extreme that they name: The residual stream's entries have scales that differ by row and by column (up to tenfold each), so neither rows nor columns share one magnitude.
All inputs are finite; a program needn't handle non-finite values.
Results may differ from a plain program's by a relative error of at most 0.0013.
Values may be sent and summed in bfloat16 or wider, within the bound.
A program may use at most 64 MiB of HBM per device.

v0:
```python
import jax
import jax.numpy as jnp
from jax import lax
from jax.sharding import PartitionSpec as P

epsilon = 1e-06


def joined(part, axis, combine):
    gathered = jax.tree.map(lambda a: lax.all_gather(a, axis), part)

    def take(source):
        return jax.tree.map(lambda a: lax.dynamic_index_in_dim(a, source, 0, False), gathered)

    return lax.fori_loop(
        1, lax.axis_size(axis), lambda source, state: combine(state, take(source)), take(0)
    )


def head_outputs(
    queries, keys_new, values_new, out_gate, decay_logit, beta_logit, decay_rate, state, norm_gain
):
    rows_here, heads_here = decay_logit.shape
    query_f = queries.astype(jnp.float32).reshape(rows_here, heads_here, -1)
    key_f = keys_new.astype(jnp.float32).reshape(rows_here, heads_here, -1)
    value_f = values_new.astype(jnp.float32).reshape(rows_here, heads_here, -1)
    gate_f = out_gate.astype(jnp.float32).reshape(rows_here, heads_here, -1)
    key_size = query_f.shape[2]
    query_n = query_f / jnp.sqrt(jnp.sum(query_f * query_f, axis=2, keepdims=True) + epsilon)
    query_n = query_n * key_size ** (-0.5)
    key_n = key_f / jnp.sqrt(jnp.sum(key_f * key_f, axis=2, keepdims=True) + epsilon)
    decay = jnp.exp(-decay_rate[None, :] * jax.nn.softplus(decay_logit))
    strength = jax.nn.sigmoid(beta_logit)
    state_query = jnp.einsum("bhk,bhkv->bhv", query_n, state, precision=lax.Precision.HIGHEST)
    state_key = jnp.einsum("bhk,bhkv->bhv", key_n, state, precision=lax.Precision.HIGHEST)
    intersection = jnp.sum(query_n * key_n, axis=2, keepdims=True)
    written = value_f - decay[..., None] * state_key
    output = decay[..., None] * state_query + strength[..., None] * intersection * written
    normed = output / jnp.sqrt(jnp.mean(output * output, axis=2, keepdims=True) + epsilon)
    result = normed * norm_gain * jax.nn.silu(gate_f)
    return result.reshape(rows_here, -1).astype(jnp.bfloat16)


def merge_stats(earlier, later):
    top = jnp.maximum(earlier[0], later[0])
    total = earlier[1] * jnp.exp(earlier[0] - top) + later[1] * jnp.exp(later[0] - top)
    return (top, total, earlier[2] + later[2])


def per_device(
    queries,
    keys_new,
    values_new,
    out_gate,
    decay_logit,
    beta_logit,
    decay_rate,
    state,
    norm_gain,
    out_proj,
    residual,
    final_gain,
    value_weight,
    lm_head,
    sampled,
):
    headout = head_outputs(
        queries,
        keys_new,
        values_new,
        out_gate,
        decay_logit,
        beta_logit,
        decay_rate,
        state,
        norm_gain,
    )
    partial_out = jnp.dot(headout, out_proj, preferred_element_type=jnp.float32)
    rows_own = residual.shape[0]
    attn = lax.psum(partial_out, "heads")
    hsum = residual.astype(jnp.float32) + attn
    rstd = 1.0 / jnp.sqrt(jnp.mean(hsum * hsum, axis=1) + epsilon)
    value = rstd * jnp.sum(hsum * final_gain * value_weight, axis=1)
    normed = (hsum * rstd[:, None] * final_gain).astype(jnp.bfloat16)
    logits = jnp.dot(
        lax.all_gather(normed, "batch", axis=0, tiled=True),
        lm_head,
        preferred_element_type=jnp.float32,
    )
    vocab_own = lm_head.shape[1]
    vocab_first = lax.axis_index(("heads", "batch")) * vocab_own
    local_ids = sampled - vocab_first
    columns = lax.broadcasted_iota(jnp.int32, logits.shape, 1)
    chosen = jnp.sum(jnp.where(columns == local_ids[:, None], logits, 0.0), axis=1)
    local_top = jnp.max(logits, axis=1)
    local_total = jnp.sum(jnp.exp(logits - local_top[:, None]), axis=1)
    top, total, chosen_all = joined(
        (local_top, local_total, chosen), ("heads", "batch"), merge_stats
    )
    every_logprob = chosen_all - (top + jnp.log(total))
    logprob = lax.dynamic_slice_in_dim(
        every_logprob, lax.axis_index("batch") * rows_own, rows_own, 0
    )
    return (logprob, value)


def solution(mesh):
    placed = (
        P("batch", "heads"),
        P("batch", "heads"),
        P("batch", "heads"),
        P("batch", "heads"),
        P("batch", "heads"),
        P("batch", "heads"),
        P("heads"),
        P("batch", "heads", None, None),
        P(),
        P("heads", None),
        P("batch", None),
        P(),
        P(),
        P(None, ("heads", "batch")),
        P(),
    )
    return jax.shard_map(
        per_device, mesh=mesh, in_specs=placed, out_specs=(P("batch"), P("batch")), check_vma=False
    )
```

profile of v0, /device:TPU:0, one launch (start us, length us, event | category | flops | bytes accessed | tf_op | source)
XLA Modules:
  0.0 143.0 jit_solution(5027682328408560421)
XLA Ops:
  7.2 0.0 copy-start
  7.2 0.0 all-reduce.6.cloned.1.call-start
  7.2 0.0 copy-start.1
  7.2 1.0 fusion.7
  8.2 1.1 fusion.9
  9.3 0.9 fusion.22
  10.3 0.0 copy-start.8
  10.3 0.0 copy-start.3
  10.3 5.3 %fusion.16 = f32[8,8,1,128]{3,2,1,0:T(1,128)S(1)} fusion(f32[8,8,128,128]{3,2,1,0:T(8,128)} %param.24, f32[8,8,128,1]{2,0,1,3:T(8,128)S(1)} %get-tuple-element.209), kind=kOutput, calls=%fused_computation.32 | convolution fusion | flops 12582912 | bytes 4259840 | tf_op jit(solution)/shard_map/bhk,bhkv->bhv/dot_general | solution.py:35
  15.6 3.7 %fusion.18 = f32[8,8,1,128]{3,2,1,0:T(1,128)S(1)} fusion(f32[8,8,128,128]{3,2,1,0:T(8,128)S(1)} %copy-done.1, f32[8,8,128,1]{2,0,1,3:T(8,128)S(1)} %get-tuple-element.207), kind=kOutput, calls=%fused_computation.34 | convolution fusion | flops 12582912 | bytes 4259840 | tf_op jit(solution)/shard_map/bhk,bhkv->bhv/dot_general | solution.py:34
  19.3 0.1 copy.20
  19.4 0.1 copy.19
  19.5 0.2 multiply_reduce_fusion.2
  19.7 0.0 copy-start.11
  19.7 5.3 %fusion.23 = f32[8,4096]{1,0:T(8,128)} fusion(bf16[1024,4096]{1,0:T(8,128)(2,1)} %param.26, bf16[8,1024]{1,0:T(8,128)(2,1)S(1)} %copy-done.5, f32[128]{0:T(128)S(1)} %copy-done.9, f32[8,8]{0,1:T(8,128)S(1)} %add_sqrt_fusion, f32[8,8,1,128]{3,2,1,0:T(1,128)S(1)} %fusion.16, f32[8,8,1,128]{3,2,1,0:T(1,128)S(1)} %fusion.18, bf16[8,1024]{1,0:T(8,128)(2,1)S(1)} %copy-done.3, ...), kind=kOutput, calls=%fused_computation.44 | convolution fusion | flops 67231744 | bytes 8619264 | tf_op jit(solution)/shard_map/dot_general | solution.py:78
  25.0 0.0 all-reduce.6.cloned.1.call-update
  25.1 34.6 %all-reduce.6.cloned.1.call-done = f32[8,4096]{1,0:T(8,128)} async-done(((f32[8,4096]{1,0:T(8,128)}), f32[8,4096]{1,0:T(8,128)}) %all-reduce.6.cloned.1.call-update) | async-done | bytes 131088 | tf_op jit(solution)/shard_map/psum | solution.py:80
  59.7 1.1 multiply_reduce_fusion
  60.8 0.5 fusion.32
  61.4 1.0 multiply_convert_fusion
  62.4 31.4 %all_gather.21 = bf16[64,4096]{1,0:T(8,128)(2,1)S(1)} all-gather(bf16[8,4096]{1,0:T(8,128)(2,1)S(1)} %multiply_convert_fusion), channel_id=1, replica_groups=mesh['heads'=4,'batch'=8] {'batch'}, dimensions={0}, use_global_device_ids=true | all-gather | bytes 589824 | tf_op jit(solution)/shard_map/all_gather | solution.py:86
  93.7 0.4 fusion.35
  94.2 0.2 select_reduce_fusion
  94.4 0.3 dynamic-update-slice
  94.7 0.3 dynamic-update-slice.2
  94.9 0.3 dynamic-update-slice.1
  95.2 38.7 %all-reduce.3 = (f32[2048]{0:T(1024)S(1)}, f32[2048]{0:T(1024)S(1)}, f32[2048]{0:T(1024)S(1)}) all-reduce(f32[2048]{0:T(1024)S(1)} %dynamic-update-slice, f32[2048]{0:T(1024)S(1)} %dynamic-update-slice.1, f32[2048]{0:T(1024)S(1)} %dynamic-update-slice.2), channel_id=2, replica_groups=mesh['heads'=4,'batch'=8] {'heads','batch'}, use_global_device_ids=true, to_apply=%add | all-reduce | flops 6144 | bytes 49152
  133.8 0.1 reshape.81
  133.9 0.1 reshape.82
  134.0 0.1 reshape.83
  134.1 1.4 %while.19 = (s32[]{:T(128)}, f32[64]{0:T(128)S(1)}, f32[64]{0:T(128)S(1)}, f32[64]{0:T(128)S(1)}, f32[32,64]{1,0:T(8,128)S(1)}, /*index=5*/f32[32,64]{1,0:T(8,12...) while((s32[]{:T(128)}, f32[64]{0:T(128)S(1)}, f32[64]{0:T(128)S(1)}, f32[64]{0:T(128)S(1)}, ...), condition=%wide.region_10.11_spmd, body=%wide.region_9.10_spmd.sunk | while | flops 453 | bytes 2451 | solution.py:15
  135.5 0.6 dynamic_slice.46
  (63 shorter events, 1.0 us)
Async XLA Ops:
  7.2 86.6 %copy-start = (bf16[4096,128]{1,0:T(8,128)(2,1)S(1)}, bf16[4096,128]{1,0:T(8,128)(2,1)}, u32[]{:S(2)}) copy-start(bf16[4096,128]{1,0:T(8,128)(2,1)} %param.30) | copy-start | bytes 3145732
  7.2 52.6 %all-reduce.6.cloned.1.call-start = ((), (), s32[]{:S(2)}) async-start(), calls=%async_computation | async-start | bytes 262144 | tf_op jit(solution)/shard_map/psum | solution.py:80
  7.2 8.4 %copy-start.1 = (f32[8,8,128,128]{3,2,1,0:T(8,128)S(1)}, f32[8,8,128,128]{3,2,1,0:T(8,128)}, u32[]{:S(2)}) copy-start(f32[8,8,128,128]{3,2,1,0:T(8,128)} %param.24) | copy-start | bytes 12582916
  10.2 9.1 %copy-start.7 = (f32[8,8]{1,0:T(8,128)S(1)}, f32[8,8]{1,0:T(8,128)}, u32[]{:S(2)}) copy-start(f32[8,8]{1,0:T(8,128)} %param.22) | copy-start | bytes 772
  10.3 9.1 %copy-start.10 = (f32[8]{0:T(128)S(1)}, f32[8]{0:T(128)}, u32[]{:S(2)}) copy-start(f32[8]{0:T(128)} %param.23) | copy-start | bytes 100
  10.3 9.1 %copy-start.8 = (f32[8,8]{1,0:T(8,128)S(1)}, f32[8,8]{1,0:T(8,128)}, u32[]{:S(2)}) copy-start(f32[8,8]{1,0:T(8,128)} %param.21) | copy-start | bytes 772
  10.3 9.2 %copy-start.3 = (bf16[8,1024]{1,0:T(8,128)(2,1)S(1)}, bf16[8,1024]{1,0:T(8,128)(2,1)}, u32[]{:S(2)}) copy-start(bf16[8,1024]{1,0:T(8,128)(2,1)} %param.19) | copy-start | bytes 49156
  10.3 9.4 %copy-start.5 = (bf16[8,1024]{1,0:T(8,128)(2,1)S(1)}, bf16[8,1024]{1,0:T(8,128)(2,1)}, u32[]{:S(2)}) copy-start(bf16[8,1024]{1,0:T(8,128)(2,1)} %param.20) | copy-start | bytes 49156
  10.3 9.4 %copy-start.9 = (f32[128]{0:T(128)S(1)}, f32[128]{0:T(128)}, u32[]{:S(2)}) copy-start(f32[128]{0:T(128)} %param.25) | copy-start | bytes 1540
  19.7 5.4 %copy-start.11 = (s32[64]{0:T(128)S(1)}, s32[64]{0:T(128)}, u32[]{:S(2)}) copy-start(s32[64]{0:T(128)} %param.31) | copy-start | bytes 772
  19.7 40.0 %copy-start.2 = (bf16[8,4096]{1,0:T(8,128)(2,1)S(1)}, bf16[8,4096]{1,0:T(8,128)(2,1)}, u32[]{:S(2)}) copy-start(bf16[8,4096]{1,0:T(8,128)(2,1)} %param.27) | copy-start | bytes 196612
  19.7 40.0 %copy-start.4 = (f32[4096]{0:T(1024)S(1)}, f32[4096]{0:T(1024)}, u32[]{:S(2)}) copy-start(f32[4096]{0:T(1024)} %param.28) | copy-start | bytes 49156
  19.7 40.0 %copy-start.6 = (f32[4096]{0:T(1024)S(1)}, f32[4096]{0:T(1024)}, u32[]{:S(2)}) copy-start(f32[4096]{0:T(1024)} %param.29) | copy-start | bytes 49156
Sparse Core Ops, SparseCore 0:
  25.2 34.4 all-reduce.5
where the time goes:
time: 144 us; the launch traced here: 143 us
  blocking collectives  70.1 us (49%)
  waiting for transfers between devices  34.6 us (24%)
  matrix products  14.7 us (10%)
  between operations  14.2 us (10%)
  other arithmetic  6.89 us (5%)
  local copies, waits for them, and re-layouts  1.82 us (1%)
    unnamed x1, blocking collectives  38.7 us
    psum x1, waiting for transfers between devices, per_device(): attn = lax.psum(partial_out, 'heads')  34.6 us
    all_gather x1, blocking collectives, per_device(): lax.all_gather(normed, 'batch', axis=0, tiled=True)  31.4 us
    dot_general x1, matrix products, head_outputs(): jnp.einsum('bhk,bhkv->bhv', key_n, state, precision=lax.Precision.HIGHEST)  5.31 us
    dot_general x1, matrix products, per_device(): partial_out = jnp.dot(headout, out_proj, preferred_element_type=jnp.float32)  5.31 us
    dot_general x1, matrix products, head_outputs(): jnp.einsum('bhk,bhkv->bhv', query_n, state, precision=lax.Precision.HIGHEST)  3.66 us
  transfers between devices with their start and end apart: 1, of which 1 were waited for; matrix products, arithmetic and copies ran while one was open for 0% of the time, Pallas kernels for 0%

commit v1 on v0

--- a/solution.py
+++ b/solution.py
@@ -77,7 +77,8 @@
     )
     partial_out = jnp.dot(headout, out_proj, preferred_element_type=jnp.float32)
     rows_own = residual.shape[0]
-    attn = lax.psum(partial_out, "heads")
+    parts = lax.all_gather(partial_out, "heads", axis=0, tiled=False)
+    attn = parts.sum(axis=0)
     hsum = residual.astype(jnp.float32) + attn
     rstd = 1.0 / jnp.sqrt(jnp.mean(hsum * hsum, axis=1) + epsilon)
     value = rstd * jnp.sum(hsum * final_gain * value_weight, axis=1)

time: 144 us -> 103 us (0.72)
  waiting for transfers between devices: 34.6 us -> 0 us
  between operations: 14.2 us -> 0.89 us
  blocking collectives: 70.1 us -> 79.7 us
  other arithmetic: 6.89 us -> 5.12 us
    psum x1 -> x0, waiting for transfers between devices: 34.6 us -> none  [per_device(): attn = lax.psum(partial_out, 'heads')]
    all_gather x0 -> x1, blocking collectives: none -> 8.67 us  [per_device(): parts = lax.all_gather(partial_out, 'heads', axis=0, tiled=False)]
  transfers between devices with their start and end apart: 1 -> 0, of which waited for: 1 -> 0; matrix products, arithmetic and copies ran while one was open for 0% -> 0% of each run, Pallas kernels for 0% -> 0%
where the time goes in v1:
time: 103 us; the launch traced here: 102 us
  blocking collectives  79.7 us (77%)
  matrix products  14 us (14%)
  other arithmetic  5.12 us (5%)
  local copies, waits for them, and re-layouts  1.82 us (2%)
    unnamed x1, blocking collectives  39.2 us
    all_gather x1, blocking collectives, per_device(): lax.all_gather(normed, 'batch', axis=0, tiled=True)  31.9 us
    all_gather x1, blocking collectives, per_device(): parts = lax.all_gather(partial_out, 'heads', axis=0, tiled=False)  8.67 us
    dot_general x1, matrix products, head_outputs(): jnp.einsum('bhk,bhkv->bhv', key_n, state, precision=lax.Precision.HIGHEST)  5.31 us
    dot_general x1, matrix products, per_device(): partial_out = jnp.dot(headout, out_proj, preferred_element_type=jnp.float32)  4.63 us
    dot_general x1, matrix products, head_outputs(): jnp.einsum('bhk,bhkv->bhv', query_n, state, precision=lax.Precision.HIGHEST)  3.66 us

profile of v1, /device:TPU:0, one launch (start us, length us, event | category | flops | bytes accessed | tf_op | source)
XLA Modules:
  0.0 102.1 jit_solution(3245902324087259836)
XLA Ops:
  0.6 0.0 copy-start
  0.6 0.0 copy-start.1
  0.7 1.0 fusion.7
  1.6 1.1 %fusion.9 = f32[8,8]{0,1:T(8,128)S(1)} fusion(bf16[8,1024]{1,0:T(8,128)(2,1)} %param.18), kind=kLoop, calls=%fused_computation.23 | loop fusion | flops 24512 | bytes 16640 | tf_op jit(solution)/shard_map/reduce_sum | solution.py:31
  2.8 0.9 fusion.22
  3.7 0.0 copy-start.7
  3.7 0.0 copy-start.3
  3.7 0.0 copy-start.5
  3.7 5.3 %fusion.16 = f32[8,8,1,128]{3,2,1,0:T(1,128)S(1)} fusion(f32[8,8,128,128]{3,2,1,0:T(8,128)} %param.24, f32[8,8,128,1]{2,0,1,3:T(8,128)S(1)} %get-tuple-element.209), kind=kOutput, calls=%fused_computation.33 | convolution fusion | flops 12582912 | bytes 4259840 | tf_op jit(solution)/shard_map/bhk,bhkv->bhv/dot_general | solution.py:35
  9.1 3.7 %fusion.18 = f32[8,8,1,128]{3,2,1,0:T(1,128)S(1)} fusion(f32[8,8,128,128]{3,2,1,0:T(8,128)S(1)} %copy-done.1, f32[8,8,128,1]{2,0,1,3:T(8,128)S(1)} %get-tuple-element.207), kind=kOutput, calls=%fused_computation.35 | convolution fusion | flops 12582912 | bytes 4259840 | tf_op jit(solution)/shard_map/bhk,bhkv->bhv/dot_general | solution.py:34
  12.7 0.1 copy.20
  12.8 0.1 copy.19
  12.9 0.2 multiply_reduce_fusion.2
  13.1 0.0 copy-start.2
  13.2 0.0 copy-start.11
  13.2 4.6 %fusion.23 = f32[8,4096]{1,0:T(8,128)S(1)} fusion(bf16[1024,4096]{1,0:T(8,128)(2,1)} %param.26, bf16[8,1024]{1,0:T(8,128)(2,1)S(1)} %copy-done.5, f32[128]{0:T(128)S(1)} %copy-done.9, f32[8,8]{0,1:T(8,128)S(1)} %add_sqrt_fusion, f32[8,8,1,128]{3,2,1,0:T(1,128)S(1)} %fusion.16, f32[8,8,1,128]{3,2,1,0:T(1,128)S(1)} %fusion.18, ...), kind=kOutput, calls=%fused_computation.45 | convolution fusion | flops 67231744 | bytes 8619264 | tf_op jit(solution)/shard_map/dot_general | solution.py:78
  17.8 8.7 %all-gather = f32[32,4096]{1,0:T(8,128)S(1)} all-gather(f32[8,4096]{1,0:T(8,128)S(1)} %fusion.23), channel_id=2, replica_groups=mesh['heads'=4,'batch'=8] {'heads'}, dimensions={0}, use_global_device_ids=true | all-gather | bytes 655360 | tf_op jit(solution)/shard_map/all_gather | solution.py:80
  26.5 0.2 multiply_reduce_fusion
  26.7 0.5 fusion.32
  27.3 0.1 multiply_convert_fusion
  27.3 31.9 %all_gather.29 = bf16[64,4096]{1,0:T(8,128)(2,1)S(1)} all-gather(bf16[8,4096]{1,0:T(8,128)(2,1)S(1)} %multiply_convert_fusion), channel_id=1, replica_groups=mesh['heads'=4,'batch'=8] {'batch'}, dimensions={0}, use_global_device_ids=true | all-gather | bytes 589824 | tf_op jit(solution)/shard_map/all_gather | solution.py:87
  59.2 0.4 fusion.35
  59.7 0.2 select_reduce_fusion
  59.9 0.3 dynamic-update-slice.2
  60.1 0.3 dynamic-update-slice.1
  60.4 0.3 dynamic-update-slice
  60.7 39.2 %all-reduce.3 = (f32[2048]{0:T(1024)S(1)}, f32[2048]{0:T(1024)S(1)}, f32[2048]{0:T(1024)S(1)}) all-reduce(f32[2048]{0:T(1024)S(1)} %dynamic-update-slice, f32[2048]{0:T(1024)S(1)} %dynamic-update-slice.1, f32[2048]{0:T(1024)S(1)} %dynamic-update-slice.2), channel_id=3, replica_groups=mesh['heads'=4,'batch'=8] {'heads','batch'}, use_global_device_ids=true, to_apply=%add | all-reduce | flops 6144 | bytes 49152
  99.8 0.1 reshape.82
  99.9 0.1 reshape.83
  100.0 0.1 reshape.84
  100.1 1.4 %while.19 = (s32[]{:T(128)}, f32[64]{0:T(128)S(1)}, f32[64]{0:T(128)S(1)}, f32[64]{0:T(128)S(1)}, f32[32,64]{1,0:T(8,128)S(1)}, /*index=5*/f32[32,64]{1,0:T(8,12...) while((s32[]{:T(128)}, f32[64]{0:T(128)S(1)}, f32[64]{0:T(128)S(1)}, f32[64]{0:T(128)S(1)}, ...), condition=%wide.region_10.11_spmd, body=%wide.region_9.10_spmd.sunk | while | flops 453 | bytes 2451 | solution.py:15
  101.5 0.6 dynamic_slice.46
  (62 shorter events, 1.0 us)
Async XLA Ops:
  0.6 58.6 %copy-start = (bf16[4096,128]{1,0:T(8,128)(2,1)S(1)}, bf16[4096,128]{1,0:T(8,128)(2,1)}, u32[]{:S(2)}) copy-start(bf16[4096,128]{1,0:T(8,128)(2,1)} %param.30) | copy-start | bytes 3145732
  0.6 8.4 %copy-start.1 = (f32[8,8,128,128]{3,2,1,0:T(8,128)S(1)}, f32[8,8,128,128]{3,2,1,0:T(8,128)}, u32[]{:S(2)}) copy-start(f32[8,8,128,128]{3,2,1,0:T(8,128)} %param.24) | copy-start | bytes 12582916
  3.7 9.1 %copy-start.7 = (f32[8,8]{1,0:T(8,128)S(1)}, f32[8,8]{1,0:T(8,128)}, u32[]{:S(2)}) copy-start(f32[8,8]{1,0:T(8,128)} %param.22) | copy-start | bytes 772
  3.7 9.1 %copy-start.10 = (f32[8]{0:T(128)S(1)}, f32[8]{0:T(128)}, u32[]{:S(2)}) copy-start(f32[8]{0:T(128)} %param.23) | copy-start | bytes 100
  3.7 9.1 %copy-start.8 = (f32[8,8]{1,0:T(8,128)S(1)}, f32[8,8]{1,0:T(8,128)}, u32[]{:S(2)}) copy-start(f32[8,8]{1,0:T(8,128)} %param.21) | copy-start | bytes 772
  3.7 9.2 %copy-start.3 = (bf16[8,1024]{1,0:T(8,128)(2,1)S(1)}, bf16[8,1024]{1,0:T(8,128)(2,1)}, u32[]{:S(2)}) copy-start(bf16[8,1024]{1,0:T(8,128)(2,1)} %param.19) | copy-start | bytes 49156
  3.7 9.4 %copy-start.5 = (bf16[8,1024]{1,0:T(8,128)(2,1)S(1)}, bf16[8,1024]{1,0:T(8,128)(2,1)}, u32[]{:S(2)}) copy-start(bf16[8,1024]{1,0:T(8,128)(2,1)} %param.20) | copy-start | bytes 49156
  3.7 9.4 %copy-start.9 = (f32[128]{0:T(128)S(1)}, f32[128]{0:T(128)}, u32[]{:S(2)}) copy-start(f32[128]{0:T(128)} %param.25) | copy-start | bytes 1540
  13.1 13.4 %copy-start.2 = (bf16[8,4096]{1,0:T(8,128)(2,1)S(1)}, bf16[8,4096]{1,0:T(8,128)(2,1)}, u32[]{:S(2)}) copy-start(bf16[8,4096]{1,0:T(8,128)(2,1)} %param.27) | copy-start | bytes 196612
  13.1 13.4 %copy-start.4 = (f32[4096]{0:T(1024)S(1)}, f32[4096]{0:T(1024)}, u32[]{:S(2)}) copy-start(f32[4096]{0:T(1024)} %param.28) | copy-start | bytes 49156
  13.1 13.4 %copy-start.6 = (f32[4096]{0:T(1024)S(1)}, f32[4096]{0:T(1024)}, u32[]{:S(2)}) copy-start(f32[4096]{0:T(1024)} %param.29) | copy-start | bytes 49156
  13.2 46.5 %copy-start.11 = (s32[64]{0:T(128)S(1)}, s32[64]{0:T(128)}, u32[]{:S(2)}) copy-start(s32[64]{0:T(128)} %param.31) | copy-start | bytes 772
